TPU v7x, 32 devices: a whole 2x2x4 slice. The times are simulated.
32 devices in a mesh: dp: 16 (over z, x, core), mp: 2 (over y).
Axes of the slice: x: 2, y: 2, z: 4, core: 2. Of those that a mesh axis runs over, the one named last changes fastest.
Arguments:
- tokens: bfloat16 [192, 4608], P('dp', 'mp'), may hold values from -6 to 6
- frozen_weight: bfloat16 [2, 4608, 36864], P(None, 'mp', 'dp'), may hold values from -36 to 36
- adapter_down: bfloat16 [2, 16, 4608], P(None, None, 'mp'), may hold values from -1.5 to 1.5
- adapter_up: bfloat16 [2, 16, 36864], P(None, None, 'dp'), may hold values from -3 to 3
- magnitude: float32 [2, 36864], P(None, 'dp'), may hold values from 0.5 to 2
- hidden_gradient: bfloat16 [192, 36864], P('mp', 'dp'), may hold values from -0.59765625 to 0.59765625
Outputs:
- hidden: bfloat16 [192, 36864], P('mp', 'dp')
- token_gradient: float32 [192, 4608], P('dp', 'mp')
- adapter_down_gradient: float32 [2, 16, 4608], P(None, None, 'mp')
- adapter_up_gradient: float32 [2, 16, 36864], P(None, None, 'dp')
- magnitude_gradient: float32 [2, 36864], P(None, 'dp')
All inputs are finite; a program needn't handle non-finite values.
Results may differ from a plain program's by a relative error of at most 0.023.
Values may be sent and summed in bfloat16 or wider, within the bound.
A program may use at most 64 MiB of HBM per device.

v0:
```python
import jax
import jax.numpy as jnp
from jax import lax
from jax.sharding import PartitionSpec as P

LOWRANK_SCALE = 2.0
EPSILON = 1e-06
MATMUL_ACCURACY = lax.Precision.HIGHEST


def gelu_pair(source):
    cubic_term = source + 0.044715 * source * source * source
    tangent = jnp.tanh(0.7978845608028654 * cubic_term)
    result = 0.5 * source * (1.0 + tangent)
    derivative = 0.5 * (1.0 + tangent) + 0.5 * source * (
        1.0 - tangent * tangent
    ) * 0.7978845608028654 * (1.0 + 0.134145 * source * source)
    return (result, derivative)


def on_device(tokens, frozen_weight, adapter_down, adapter_up, magnitude, hidden_gradient):
    every_row = lax.all_gather(tokens, "dp", axis=0, tiled=True)
    down_broad = adapter_down.astype(jnp.float32)
    up_broad = adapter_up.astype(jnp.float32)
    base_square = jnp.sum(jnp.square(frozen_weight.astype(jnp.float32)), axis=1)
    cross_base = jnp.einsum(
        "krd,kdf->krf", adapter_down, frozen_weight, preferred_element_type=jnp.float32
    )
    gram_part = jnp.einsum(
        "krd,ksd->krs", adapter_down, adapter_down, preferred_element_type=jnp.float32
    )
    square_base, cross_total, gram_sum = (
        lax.psum(base_square.astype(jnp.bfloat16), "mp").astype(jnp.float32),
        lax.psum(cross_base.astype(jnp.bfloat16), "mp").astype(jnp.float32),
        lax.psum(gram_part.astype(jnp.bfloat16), "mp").astype(jnp.float32),
    )
    gram_up = jnp.einsum("krs,ksf->krf", gram_sum, up_broad, precision=MATMUL_ACCURACY)
    mixed_sum = cross_total + LOWRANK_SCALE * gram_up
    square_sum = (
        square_base
        + 2.0 * LOWRANK_SCALE * jnp.sum(up_broad * cross_total, axis=1)
        + LOWRANK_SCALE * LOWRANK_SCALE * jnp.sum(up_broad * gram_up, axis=1)
    )
    base_part = jnp.einsum(
        "td,kdf->ktf", every_row, frozen_weight, preferred_element_type=jnp.float32
    )
    lowrank_piece = jnp.einsum(
        "su,vgu->vsg", every_row, adapter_down, preferred_element_type=jnp.float32
    )
    col_norm = jnp.sqrt(square_sum + EPSILON)
    col_ratio = magnitude / col_norm
    share_rows = every_row.shape[0] // lax.axis_size("mp")
    base_sum, low_sum = (
        lax.psum(base_part.astype(jnp.bfloat16), "mp").astype(jnp.float32),
        lax.psum(lowrank_piece.astype(jnp.bfloat16), "mp").astype(jnp.float32),
    )
    cot_rows = lax.all_gather(hidden_gradient, "mp", axis=0, tiled=True)
    token_lowrank = low_sum.astype(jnp.bfloat16)
    unscaled_output = base_sum + LOWRANK_SCALE * jnp.einsum(
        "hls,hse->hle", token_lowrank, adapter_up, preferred_element_type=jnp.float32
    )
    gate_proj = unscaled_output[0] * col_ratio[0]
    up_proj = unscaled_output[1] * col_ratio[1]
    activated, derivative = gelu_pair(gate_proj)
    hidden_rows = (activated * up_proj).astype(jnp.bfloat16)
    cotangent = cot_rows.astype(jnp.float32)
    grad_out = jnp.stack([cotangent * up_proj * derivative, cotangent * activated])
    moment_part = jnp.sum(grad_out * unscaled_output, axis=1)
    prescale_gradient = (grad_out * col_ratio[:, None, :]).astype(jnp.bfloat16)
    lowrank_gradient_piece = jnp.einsum(
        "hmu,hmq->huq", token_lowrank, prescale_gradient, preferred_element_type=jnp.float32
    )
    hidden = lax.dynamic_slice_in_dim(hidden_rows, lax.axis_index("mp") * share_rows, share_rows, 0)
    magnitude_gradient = moment_part / col_norm
    frozen_term = -magnitude * moment_part / (col_norm * col_norm * col_norm)
    adapter_up_gradient = LOWRANK_SCALE * (
        lowrank_gradient_piece + mixed_sum * frozen_term[:, None, :]
    )
    lowrank_gradient = jnp.einsum(
        "pge,pbe->pgb", prescale_gradient, adapter_up, preferred_element_type=jnp.float32
    ).astype(jnp.bfloat16)
    weighted_adapter_up = up_broad * frozen_term[:, None, :]
    broadcast_value = jnp.einsum(
        "krf,kdf->krd",
        weighted_adapter_up,
        frozen_weight.astype(jnp.float32),
        precision=MATMUL_ACCURACY,
    )
    inner_gram = jnp.einsum(
        "krf,ksf->krs", weighted_adapter_up, up_broad, precision=MATMUL_ACCURACY
    )
    broadcast_value = broadcast_value + LOWRANK_SCALE * jnp.einsum(
        "krs,ksd->krd", inner_gram, down_broad, precision=MATMUL_ACCURACY
    )
    down_piece = LOWRANK_SCALE * (
        jnp.einsum("ijp,jv->ipv", lowrank_gradient, every_row, preferred_element_type=jnp.float32)
        + broadcast_value
    )
    adapter_down_gradient = lax.psum(down_piece, "dp")
    main_term = jnp.einsum(
        "ktf,kdf->td", prescale_gradient, frozen_weight, preferred_element_type=jnp.float32
    )
    token_gradient = lax.psum_scatter(
        main_term
        + LOWRANK_SCALE
        * jnp.einsum(
            "ijf,ifh->jh", lowrank_gradient, adapter_down, preferred_element_type=jnp.float32
        ),
        "dp",
        scatter_dimension=0,
        tiled=True,
    )
    return (hidden, token_gradient, adapter_down_gradient, adapter_up_gradient, magnitude_gradient)


def solution(mesh):
    in_specs = (
        P("dp", "mp"),
        P(None, "mp", "dp"),
        P(None, None, "mp"),
        P(None, None, "dp"),
        P(None, "dp"),
        P("mp", "dp"),
    )
    out_specs = (
        P("mp", "dp"),
        P("dp", "mp"),
        P(None, None, "mp"),
        P(None, None, "dp"),
        P(None, "dp"),
    )
    return jax.shard_map(
        on_device, mesh=mesh, in_specs=in_specs, out_specs=out_specs, check_vma=False
    )
```

profile of v0, /device:TPU:0, one launch (start us, length us, event | category | flops | bytes accessed | tf_op | source)
XLA Modules:
  0.0 308.0 jit_solution(16763437248531426310)
XLA Ops:
  7.2 0.0 copy-start
  7.2 0.0 all-reduce.9.cloned.1.call-start
  7.2 26.6 %all-gather = bf16[16,12,2304]{2,1,0:T(8,128)(2,1)S(1)} all-gather(bf16[1,12,2304]{2,1,0:T(8,128)(2,1)} %bitcast.66), channel_id=1, replica_groups=mesh['dp'=16,'mp'=2] {'dp'}, dimensions={0}, use_global_device_ids=true | all-gather | bytes 940032 | tf_op jit(solution)/shard_map/all_gather | solution.py:22
  33.9 0.2 reshape.14
  34.1 0.0 copy-start.1
  34.1 12.7 %fusion.2 = bf16[2,192,2304]{2,1,0:T(8,128)(2,1)} fusion(bf16[192,2304,1]{1,0,2:T(8,128)(2,1)S(1)} %reshape.14, bf16[2,2304,2304]{2,1,0:T(8,128)(2,1)} %param.7), kind=kOutput, calls=%fused_computation.4 | convolution fusion | flops 4077748224 | bytes 23887872 | tf_op jit(solution)/shard_map/td,kdf->ktf/dot_general | solution.py:44
  46.8 0.0 copy-done
  46.8 1.0 copy-done.1
  47.8 3.5 %convolution_convert_fusion.1 = bf16[2,16,2304]{2,1,0:T(8,128)(2,1)} fusion(bf16[2,16,2304]{2,1,0:T(8,128)(2,1)S(1)} %copy-done, bf16[2,2304,2304]{2,1,0:T(8,128)(2,1)S(1)} %copy-done.1), kind=kOutput, calls=%fused_computation.18 | convolution fusion | flops 339812352 | bytes 21528576 | tf_op jit(solution)/shard_map/krd,kdf->krf/dot_general | solution.py:26
  51.3 0.0 copy-start.8
  51.3 0.0 all-reduce.9.cloned.1.call-update
  51.3 0.0 all-reduce.7.cloned.1.call-start
  51.4 0.2 convolution_convert_fusion.4
  51.6 0.4 copy-done.8
  52.0 0.6 dynamic-slice.4
  53.2 0.3 fusion.18
  53.6 0.0 copy-start.4
  53.6 0.0 copy-start.2
  53.6 9.3 %multiply_reduce_fusion = bf16[2,2304]{1,0:T(2,128)(2,1)S(1)} fusion(bf16[2,2304,2304]{2,1,0:T(8,128)(2,1)} %param.7), kind=kLoop, calls=%fused_computation | loop fusion | flops 31845888 | bytes 21242880 | tf_op jit(solution)/shard_map/reduce_sum | solution.py:25
  62.9 0.0 copy-start.5
  62.9 9.7 %all-reduce.2 = (bf16[2,192,16]{1,2,0:T(8,128)(2,1)S(1)}, bf16[2,16,16]{2,1,0:T(8,128)(2,1)S(1)}, bf16[2,2304]{1,0:T(2,128)(2,1)S(1)}) all-reduce(bf16[2,192,16]{1,2,0:T(8,128)(2,1)S(1)} %fusion.18, bf16[2,16,16]{2,1,0:T(8,128)(2,1)S(1)} %convolution_convert_fusion.4, ...), channel_id=1, replica_groups=mesh['dp'=16,'mp'=2] {'mp'}, use_global_device_ids=true, to_apply=%region_1.0 | all-reduce | flops 11264 | bytes 45056 | tf_op jit(solution)/shard_map/psum | solution.py:55
  72.7 0.0 copy-done.4
  72.7 0.0 copy-start.6
  72.7 14.4 %all_gather.7 = bf16[192,2304]{1,0:T(8,128)(2,1)S(1)} all-gather(bf16[96,2304]{1,0:T(8,128)(2,1)S(1)} %copy-done.4), channel_id=1, replica_groups=mesh['dp'=16,'mp'=2] {'mp'}, dimensions={0}, use_global_device_ids=true | all-gather | bytes 1327104 | tf_op jit(solution)/shard_map/all_gather | solution.py:57
  87.1 29.1 %all-reduce.9.cloned.1.call-done = (bf16[2,192,2304]{2,1,0:T(8,128)(2,1)}, bf16[2,16,2304]{2,1,0:T(8,128)(2,1)}) async-done(((bf16[2,192,2304]{2,1,0:T(8,128)(2,1)}, bf16[2,16,2304]{2,1,0:T(8,128)(2,1)}), (bf16[2,192,2304]{2,1,0:T(8,128)(2,1)}, bf16[2,16,2304]{2,1,0:T(8,128)(2,1)})) %all-reduce.9.cloned.1.call-update) | async-done | bytes 1916944 | tf_op jit(solution)/shard_map/psum | solution.py:54
  116.1 0.0 copy-done.2
  116.1 1.1 fusion.22
  117.2 0.0 copy-done.5
  117.3 0.7 fusion.28
  118.0 2.1 fusion.1
  120.1 0.0 copy-done.6
  120.1 3.2 %fusion.10 = (f32[1,192,2304]{2,1,0:T(8,128)S(1)}, f32[192,2304]{1,0:T(8,128)}, f32[1,192,2304]{2,1,0:T(8,128)S(1)}, f32[192,2304]{1,0:T(8,128)}) fusion(bf16[192,2304]{1,0:T(8,128)(2,1)S(1)} %all_gather.7, f32[2304]{0:T(1024)S(1)} %get-tuple-element.7, f32[2,192,2304]{2,1,0:T(8,128)S(1)} %fusion.1, f32[2304]{0:T(1024)S(1)} %get-tuple-element.8), kind=kLoop, calls=%fused_computation.25 | loop fusion | flops 10616832 | bytes 11520000 | tf_op jit(solution)/shard_map/stack | solution.py:67
  123.3 1.1 multiply_reduce_fusion.1
  124.4 11.2 %convolution_bitcast_fusion = f32[192,2304]{1,0:T(8,128)S(1)} fusion(bf16[2,192,2304]{2,1,0:T(8,128)(2,1)S(1)} %get-tuple-element.23, bf16[2,2304,2304]{2,1,0:T(8,128)(2,1)} %param.7), kind=kOutput, calls=%fused_computation.5 | convolution fusion | flops 4076863488 | bytes 24772608 | tf_op jit(solution)/shard_map/ktf,kdf->td/dot_general | solution.py:100
  135.7 0.6 convolution_convert_fusion.2
  136.2 1.7 fusion.4
  137.9 41.5 %fusion = f32[16,2304]{1,0:T(8,128)S(1)} fusion(f32[192,2304]{1,0:T(8,128)} %fusion.4), kind=kCustom, calls=%all-reduce-scatter | all-reduce-scatter fusion | flops 589825 | bytes 1917440
  179.3 0.7 slice.20
  180.0 1.3 collective-permute-start.2
  181.3 2.0 collective-permute-start.1
  183.3 1.9 collective-permute-start
  185.2 0.3 fusion.30
  185.5 1.3 collective-permute-start.3
  186.8 1.4 fusion.29
  188.2 0.3 fusion.20
  188.5 0.3 convolution_multiply_fusion.1
  188.8 20.5 %fusion.7 = f32[2,16,2304]{2,1,0:T(8,128)} fusion(f32[2,16,2304]{2,1,0:T(8,128)S(1)} %fusion.30, f32[2,16,2304]{2,1,0:T(8,128)S(1)} %convolution_multiply_fusion.1, bf16[2,2304,2304]{2,1,0:T(8,128)(2,1)} %param.7, bf16[2,16,2304]{2,1,0:T(8,128)(2,1)S(1)} %copy-done.2, f32[2,2304]{1,0:T(2,128)S(1)} %get-tuple-element.25), kind=kOutput, calls=%fused_computation.17 | convolution fusion | flops 2038800384 | bytes 22284288 | tf_op jit(solution)/shard_map/krf,kdf->krd/dot_general | solution.py:83
  209.3 0.0 copy-start.3
  209.3 0.0 copy-start.7
  209.3 0.0 all-reduce.7.cloned.1.call-update
  209.4 2.3 fusion.19
  211.7 0.0 copy-done.3
  211.7 0.0 copy-done.7
  211.7 1.1 fusion.5
  212.8 0.0 collective-permute-done.3
  212.8 0.0 collective-permute-done.2
  212.8 0.0 collective-permute-done.1
  212.8 0.0 collective-permute-done
  212.8 2.5 concatenate
  215.3 0.7 constant_dynamic-slice_fusion
  215.9 83.6 %all-reduce.7.cloned.1.call-done = f32[2,16,2304]{2,1,0:T(8,128)} async-done(((f32[2,16,2304]{2,1,0:T(8,128)}), f32[2,16,2304]{2,1,0:T(8,128)}) %all-reduce.7.cloned.1.call-update) | async-done | bytes 294928 | tf_op jit(solution)/shard_map/psum | solution.py:99
  299.5 1.7 copy.14
  (1 shorter events, 0.0 us)
Async XLA Ops:
  7.2 39.6 %copy-start = (bf16[2,16,2304]{2,1,0:T(8,128)(2,1)S(1)}, bf16[2,16,2304]{2,1,0:T(8,128)(2,1)}, u32[]{:S(2)}) copy-start(bf16[2,16,2304]{2,1,0:T(8,128)(2,1)} %param.8) | copy-start | bytes 442372
  7.2 108.9 %all-reduce.9.cloned.1.call-start = ((), (), s32[]{:S(2)}) async-start(), calls=%async_computation.1 | async-start | bytes 3833856 | tf_op jit(solution)/shard_map/psum | solution.py:54
  34.1 13.7 %copy-start.1 = (bf16[2,2304,2304]{2,1,0:T(8,128)(2,1)S(1)}, bf16[2,2304,2304]{2,1,0:T(8,128)(2,1)}, u32[]{:S(2)}) copy-start(bf16[2,2304,2304]{2,1,0:T(8,128)(2,1)} %param.7) | copy-start | bytes 63700996
  51.3 0.7 copy-start.8
  51.3 248.1 %all-reduce.7.cloned.1.call-start = ((), (), s32[]{:S(2)}) async-start(), calls=%async_computation | async-start | bytes 589824 | tf_op jit(solution)/shard_map/psum | solution.py:99
  53.6 19.1 %copy-start.4 = (bf16[96,2304]{1,0:T(8,128)(2,1)S(1)}, bf16[96,2304]{1,0:T(8,128)(2,1)}, u32[]{:S(2)}) copy-start(bf16[96,2304]{1,0:T(8,128)(2,1)} %param.11) | copy-start | bytes 1327108
  53.6 62.5 %copy-start.2 = (bf16[2,16,2304]{2,1,0:T(8,128)(2,1)S(1)}, bf16[2,16,2304]{2,1,0:T(8,128)(2,1)}, u32[]{:S(2)}) copy-start(bf16[2,16,2304]{2,1,0:T(8,128)(2,1)} %param.9) | copy-start | bytes 442372
  62.9 54.4 %copy-start.5 = (f32[2,2304]{1,0:T(2,128)S(1)}, f32[2,2304]{1,0:T(2,128)}, u32[]{:S(2)}) copy-start(f32[2,2304]{1,0:T(2,128)} %param.10) | copy-start | bytes 55300
  72.7 47.4 %copy-start.6 = (bf16[2,192,16]{1,2,0:T(8,128)(2,1)}, bf16[2,192,16]{1,2,0:T(8,128)(2,1)S(1)}, u32[]{:S(2)}) copy-start(bf16[2,192,16]{1,2,0:T(8,128)(2,1)S(1)} %get-tuple-element.9) | copy-start | bytes 36868
  180.0 32.7 %collective-permute-start.2 = (f32[16,2304]{1,0:T(8,128)S(1)}, f32[16,2304]{1,0:T(8,128)S(1)}, u32[]{:S(2)}, u32[]{:S(2)}) collective-permute-start(f32[16,2304]{1,0:T(8,128)S(1)} %fusion), channel_id=1, source_target_pairs={{0,6},{2,8},{4,10},{6,12},{8,14},{10,16},{12,18},{14,20},{16,22},{... | collective-permute-start | bytes 442376
  181.3 31.4 %collective-permute-start.1 = (f32[16,2304]{1,0:T(8,128)S(1)}, f32[16,2304]{1,0:T(8,128)}, u32[]{:S(2)}, u32[]{:S(2)}) collective-permute-start(f32[16,2304]{1,0:T(8,128)S(1)} %fusion), channel_id=1, source_target_pairs={{0,4},{2,6},{4,8},{6,10},{8,12},{10,14},{12,16},{14,18},{16,20},{1... | collective-permute-start | bytes 442376
  183.3 29.5 %collective-permute-start = (f32[16,2304]{1,0:T(8,128)S(1)}, f32[16,2304]{1,0:T(8,128)}, u32[]{:S(2)}, u32[]{:S(2)}) collective-permute-start(f32[16,2304]{1,0:T(8,128)S(1)} %fusion), channel_id=1, source_target_pairs={{0,2},{2,4},{4,6},{6,8},{8,10},{10,12},{12,14},{14,16},{16,18},{18... | collective-permute-start | bytes 442376
  185.5 27.2 %collective-permute-start.3 = (f32[12,2304]{1,0:T(8,128)}, f32[12,2304]{1,0:T(8,128)S(1)}, u32[]{:S(2)}, u32[]{:S(2)}) collective-permute-start(f32[12,2304]{1,0:T(8,128)} %slice.20), channel_id=1, source_target_pairs={{0,8},{2,10},{4,12},{6,14},{8,16},{10,18},{12,20},{14,22},{16,24},... | collective-permute-start | bytes 331784
  209.3 2.4 copy-start.3
  209.3 2.4 copy-start.7
Sparse Core Ops, SparseCore 0:
  51.5 64.5 all-reduce.8
  209.5 89.9 all-reduce.6
where the time goes:
time: 309 us; the launch traced here: 308 us
  waiting for transfers between devices  113 us (37%)
  blocking collectives  92.2 us (30%)
  matrix products  55.8 us (18%)
  other arithmetic  18 us (6%)
  between operations  14.9 us (5%)
  local copies, waits for them, and re-layouts  7.86 us (3%)
  starting transfers between devices  6.56 us (2%)
    psum x1, waiting for transfers between devices, on_device(): adapter_down_gradient = lax.psum(down_piece, 'dp')  83.6 us
    unnamed x1, blocking collectives  41.5 us
    psum x1, waiting for transfers between devices, on_device(): lax.psum(base_part.astype(jnp.bfloat16), 'mp').astype(jnp.float32)  29.1 us
    all_gather x1, blocking collectives, on_device(): every_row = lax.all_gather(tokens, 'dp', axis=0, tiled=True)  26.6 us
    dot_general x1, matrix products, on_device(): jnp.einsum('krf,kdf->krd', weighted_adapter_up, frozen_weight.astype(jnp....  20.5 us
    all_gather x1, blocking collectives, on_device(): cot_rows = lax.all_gather(hidden_gradient, 'mp', axis=0, tiled=True)  14.4 us
    dot_general x1, matrix products, on_device(): jnp.einsum('td,kdf->ktf', every_row, frozen_weight, preferred_element_typ...  12.7 us
    dot_general x1, matrix products, on_device(): jnp.einsum('ktf,kdf->td', prescale_gradient, frozen_weight, preferred_ele...  11.2 us
  transfers between devices with their start and end apart: 6, of which 2 were waited for; matrix products, arithmetic and copies ran while one was open for 13% of the time, Pallas kernels for 0%

commit v1 on v0

--- a/solution.py
+++ b/solution.py
@@ -96,7 +96,7 @@
         jnp.einsum("ijp,jv->ipv", lowrank_gradient, every_row, preferred_element_type=jnp.float32)
         + broadcast_value
     )
-    adapter_down_gradient = lax.psum(down_piece, "dp")
+    adapter_down_gradient = jnp.sum(lax.all_gather(down_piece, "dp"), axis=0)
     main_term = jnp.einsum(
         "ktf,kdf->td", prescale_gradient, frozen_weight, preferred_element_type=jnp.float32
     )

time: 309 us -> 235 us (0.76)
  waiting for transfers between devices: 113 us -> 30.5 us
  blocking collectives: 92.2 us -> 99.1 us
  starting transfers between devices: 6.56 us -> 11.2 us
  local copies, waits for them, and re-layouts: 7.86 us -> 3.36 us
    psum x1 -> x0, waiting for transfers between devices: 83.6 us -> none  [on_device(): adapter_down_gradient = lax.psum(down_piece, 'dp')]
    unnamed x1, blocking collectives: 41.5 us -> 46.9 us
    unnamed x4, starting transfers between devices: 6.48 us -> 11.1 us
    unnamed x24 -> x19, local copies, waits for them, and re-layouts: 7.81 us -> 3.31 us
    reduce_sum x0 -> x1, other arithmetic: none -> 3.29 us  [on_device(): adapter_down_gradient = jnp.sum(lax.all_gather(down_piece, 'dp'), axis=0)]
  transfers between devices with their start and end apart: 6 -> 6, of which waited for: 2 -> 1; matrix products, arithmetic and copies ran while one was open for 13% -> 32% of each run, Pallas kernels for 0% -> 0%
where the time goes in v1:
time: 235 us; the launch traced here: 234 us
  blocking collectives  99.1 us (42%)
  matrix products  56 us (24%)
  waiting for transfers between devices  30.5 us (13%)
  other arithmetic  19.4 us (8%)
  between operations  14.9 us (6%)
  starting transfers between devices  11.2 us (5%)
  local copies, waits for them, and re-layouts  3.36 us (1%)
    unnamed x1, blocking collectives  46.9 us
    psum x1, waiting for transfers between devices, on_device(): lax.psum(base_part.astype(jnp.bfloat16), 'mp').astype(jnp.float32)  30.5 us
    all_gather x1, blocking collectives, on_device(): every_row = lax.all_gather(tokens, 'dp', axis=0, tiled=True)  26.6 us
    dot_general x1, matrix products, on_device(): jnp.einsum('krf,kdf->krd', weighted_adapter_up, frozen_weight.astype(jnp....  20.5 us
    all_gather x1, blocking collectives, on_device(): cot_rows = lax.all_gather(hidden_gradient, 'mp', axis=0, tiled=True)  16.1 us
    dot_general x1, matrix products, on_device(): jnp.einsum('td,kdf->ktf', every_row, frozen_weight, preferred_element_typ...  12.7 us
    dot_general x1, matrix products, on_device(): jnp.einsum('ktf,kdf->td', prescale_gradient, frozen_weight, preferred_ele...  11.2 us
    unnamed x4, starting transfers between devices  11.1 us
  transfers between devices with their start and end apart: 6, of which 1 were waited for; matrix products, arithmetic and copies ran while one was open for 32% of the time, Pallas kernels for 0%

profile of v1, /device:TPU:0, one launch (start us, length us, event | category | flops | bytes accessed | tf_op | source)
XLA Modules:
  0.0 234.5 jit_solution(13715816120449273330)
XLA Ops:
  7.2 0.0 copy-start
  7.2 0.0 all-reduce.6.cloned.1.call-start
  7.2 26.6 %all-gather.1 = bf16[16,12,2304]{2,1,0:T(8,128)(2,1)S(1)} all-gather(bf16[1,12,2304]{2,1,0:T(8,128)(2,1)} %bitcast.68), channel_id=1, replica_groups=mesh['dp'=16,'mp'=2] {'dp'}, dimensions={0}, use_global_device_ids=true | all-gather | bytes 940032 | tf_op jit(solution)/shard_map/all_gather | solution.py:22
  33.9 0.2 reshape.15
  34.1 0.0 copy-start.1
  34.1 12.7 %fusion.2 = bf16[2,192,2304]{2,1,0:T(8,128)(2,1)} fusion(bf16[192,2304,1]{1,0,2:T(8,128)(2,1)S(1)} %reshape.15, bf16[2,2304,2304]{2,1,0:T(8,128)(2,1)} %param.7), kind=kOutput, calls=%fused_computation.4 | convolution fusion | flops 4077748224 | bytes 23887872 | tf_op jit(solution)/shard_map/td,kdf->ktf/dot_general | solution.py:44
  46.8 0.0 copy-done
  46.8 1.0 copy-done.1
  47.8 3.5 %convolution_convert_fusion.1 = bf16[2,16,2304]{2,1,0:T(8,128)(2,1)} fusion(bf16[2,16,2304]{2,1,0:T(8,128)(2,1)S(1)} %copy-done, bf16[2,2304,2304]{2,1,0:T(8,128)(2,1)S(1)} %copy-done.1), kind=kOutput, calls=%fused_computation.18 | convolution fusion | flops 339812352 | bytes 21528576 | tf_op jit(solution)/shard_map/krd,kdf->krf/dot_general | solution.py:26
  51.3 0.0 all-reduce.6.cloned.1.call-update
  51.3 0.0 all-gather.4.cloned.1.call-start
  51.4 0.2 convolution_convert_fusion.4
  51.5 0.4 fusion.18
  51.9 0.0 copy-start.4
  51.9 0.0 copy-start.2
  52.0 9.4 %multiply_reduce_fusion = bf16[2,2304]{1,0:T(2,128)(2,1)S(1)} fusion(bf16[2,2304,2304]{2,1,0:T(8,128)(2,1)} %param.7), kind=kLoop, calls=%fused_computation | loop fusion | flops 31845888 | bytes 21242880 | tf_op jit(solution)/shard_map/reduce_sum | solution.py:25
  61.4 0.0 copy-start.5
  61.4 9.5 %all-reduce.2 = (bf16[2,192,16]{1,2,0:T(8,128)(2,1)S(1)}, bf16[2,16,16]{2,1,0:T(8,128)(2,1)S(1)}, bf16[2,2304]{1,0:T(2,128)(2,1)S(1)}) all-reduce(bf16[2,192,16]{1,2,0:T(8,128)(2,1)S(1)} %fusion.18, bf16[2,16,16]{2,1,0:T(8,128)(2,1)S(1)} %convolution_convert_fusion.4, ...), channel_id=1, replica_groups=mesh['dp'=16,'mp'=2] {'mp'}, use_global_device_ids=true, to_apply=%region_1.0 | all-reduce | flops 11264 | bytes 45056 | tf_op jit(solution)/shard_map/psum | solution.py:55
  71.0 0.0 copy-done.4
  71.0 16.1 %all_gather.13 = bf16[192,2304]{1,0:T(8,128)(2,1)S(1)} all-gather(bf16[96,2304]{1,0:T(8,128)(2,1)S(1)} %copy-done.4), channel_id=1, replica_groups=mesh['dp'=16,'mp'=2] {'mp'}, dimensions={0}, use_global_device_ids=true | all-gather | bytes 1327104 | tf_op jit(solution)/shard_map/all_gather | solution.py:57
  87.1 30.5 %all-reduce.6.cloned.1.call-done = (bf16[2,192,2304]{2,1,0:T(8,128)(2,1)}, bf16[2,16,2304]{2,1,0:T(8,128)(2,1)}) async-done(((bf16[2,192,2304]{2,1,0:T(8,128)(2,1)}, bf16[2,16,2304]{2,1,0:T(8,128)(2,1)}), (bf16[2,192,2304]{2,1,0:T(8,128)(2,1)}, bf16[2,16,2304]{2,1,0:T(8,128)(2,1)})) %all-reduce.6.cloned.1.call-update) | async-done | bytes 1916944 | tf_op jit(solution)/shard_map/psum | solution.py:54
  117.5 0.0 copy-done.2
  117.5 1.1 fusion.22
  118.7 0.0 copy-done.5
  118.7 0.1 fusion.28
  118.7 0.1 slice_reduce_fusion.1
  118.8 2.1 fusion.1
  120.9 3.2 %fusion.10 = (f32[1,192,2304]{2,1,0:T(8,128)S(1)}, f32[192,2304]{1,0:T(8,128)}, f32[1,192,2304]{2,1,0:T(8,128)S(1)}, f32[192,2304]{1,0:T(8,128)}) fusion(bf16[192,2304]{1,0:T(8,128)(2,1)S(1)} %all_gather.13, f32[2304]{0:T(1024)S(1)} %get-tuple-element.7, f32[2,192,2304]{2,1,0:T(8,128)S(1)} %fusion.1, f32[2304]{0:T(1024)S(1)} %get-tuple-element.8), kind=kLoop, calls=%fused_computation.25 | loop fusion | flops 10616832 | bytes 11520000 | tf_op jit(solution)/shard_map/stack | solution.py:67
  124.1 0.5 multiply_reduce_fusion.1
  124.6 0.6 convolution_convert_fusion.2
  125.2 0.3 fusion.30
  125.5 0.6 fusion.29
  126.1 0.3 fusion.20
  126.5 0.3 convolution_multiply_fusion.1
  126.7 0.0 copy-start.6
  126.8 20.5 %fusion.7 = f32[2,16,2304]{2,1,0:T(8,128)} fusion(f32[2,16,2304]{2,1,0:T(8,128)S(1)} %fusion.30, f32[2,16,2304]{2,1,0:T(8,128)S(1)} %convolution_multiply_fusion.1, bf16[2,2304,2304]{2,1,0:T(8,128)(2,1)} %param.7, bf16[2,16,2304]{2,1,0:T(8,128)(2,1)S(1)} %copy-done.2, f32[2,2304]{1,0:T(2,128)S(1)} %get-tuple-element.25), kind=kOutput, calls=%fused_computation.17 | convolution fusion | flops 2038800384 | bytes 22284288 | tf_op jit(solution)/shard_map/krf,kdf->krd/dot_general | solution.py:83
  147.3 0.0 all-gather.4.cloned.1.call-update
  147.3 0.0 copy-done.6
  147.3 0.6 dynamic-slice.4
  148.6 11.2 %convolution_bitcast_fusion = f32[192,2304]{1,0:T(8,128)S(1)} fusion(bf16[2,192,2304]{2,1,0:T(8,128)(2,1)S(1)} %get-tuple-element.23, bf16[2,2304,2304]{2,1,0:T(8,128)(2,1)} %param.7), kind=kOutput, calls=%fused_computation.5 | convolution fusion | flops 4076863488 | bytes 24772608 | tf_op jit(solution)/shard_map/ktf,kdf->td/dot_general | solution.py:100
  159.8 1.7 fusion.4
  161.5 0.0 copy-start.3
  161.5 46.9 %fusion = f32[16,2304]{1,0:T(8,128)S(1)} fusion(f32[192,2304]{1,0:T(8,128)} %fusion.4), kind=kCustom, calls=%all-reduce-scatter | all-reduce-scatter fusion | flops 589825 | bytes 1917440
  208.4 1.3 collective-permute-start.2
  209.7 2.7 %collective-permute-start.1 = (f32[16,2304]{1,0:T(8,128)S(1)}, f32[16,2304]{1,0:T(8,128)S(1)}, u32[]{:S(2)}, u32[]{:S(2)}) collective-permute-start(f32[16,2304]{1,0:T(8,128)S(1)} %fusion), channel_id=1, source_target_pairs={{0,4},{2,6},{4,8},{6,10},{8,12},{10,14},{12,16},{14,18},{16,20},{1... | collective-permute-start | bytes 442376
  212.5 2.9 %collective-permute-start = (f32[16,2304]{1,0:T(8,128)S(1)}, f32[16,2304]{1,0:T(8,128)S(1)}, u32[]{:S(2)}, u32[]{:S(2)}) collective-permute-start(f32[16,2304]{1,0:T(8,128)S(1)} %fusion), channel_id=1, source_target_pairs={{0,2},{2,4},{4,6},{6,8},{8,10},{10,12},{12,14},{14,16},{16,18},{18... | collective-permute-start | bytes 442376
  215.4 4.1 %collective-permute-start.3 = (f32[12,2304]{1,0:T(8,128)S(1)}, f32[12,2304]{1,0:T(8,128)S(1)}, u32[]{:S(2)}, u32[]{:S(2)}) collective-permute-start(f32[12,2304]{1,0:T(8,128)S(1)} %slice.20), channel_id=1, source_target_pairs={{0,8},{2,10},{4,12},{6,14},{8,16},{10,18},{12,20},{14,22},{16,24},... | collective-permute-start | bytes 331784
  219.5 2.3 fusion.19
  221.8 0.0 copy-done.3
  221.8 1.1 fusion.5
  222.9 0.0 collective-permute-done.3
  222.9 0.0 collective-permute-done.2
  222.9 0.0 collective-permute-done.1
  222.9 0.0 collective-permute-done
  222.9 0.8 concatenate
  223.7 0.7 constant_dynamic-slice_fusion
  224.4 0.0 all-gather.4.cloned.1.call-done
  224.4 3.3 %reduce_sum.49 = f32[2,16,2304]{2,1,0:T(8,128)} reduce(f32[16,2,16,2304]{3,2,1,0:T(8,128)} %bitcast.67, f32[]{:T(128)} %constant.14.clone.1), dimensions={0}, to_apply=%region_10.0 | reduce | flops 1105920 | bytes 5013508 | tf_op jit(solution)/shard_map/reduce_sum | solution.py:99
  (1 shorter events, 0.0 us)
Async XLA Ops:
  7.2 39.6 %copy-start = (bf16[2,16,2304]{2,1,0:T(8,128)(2,1)S(1)}, bf16[2,16,2304]{2,1,0:T(8,128)(2,1)}, u32[]{:S(2)}) copy-start(bf16[2,16,2304]{2,1,0:T(8,128)(2,1)} %param.8) | copy-start | bytes 442372
  7.2 110.4 %all-reduce.6.cloned.1.call-start = ((), (), s32[]{:S(2)}) async-start(), calls=%async_computation.1 | async-start | bytes 3833856 | tf_op jit(solution)/shard_map/psum | solution.py:54
  34.1 13.7 %copy-start.1 = (bf16[2,2304,2304]{2,1,0:T(8,128)(2,1)S(1)}, bf16[2,2304,2304]{2,1,0:T(8,128)(2,1)}, u32[]{:S(2)}) copy-start(bf16[2,2304,2304]{2,1,0:T(8,128)(2,1)} %param.7) | copy-start | bytes 63700996
  51.3 173.0 %all-gather.4.cloned.1.call-start = ((), (), s32[]{:S(2)}) async-start(), calls=%async_computation | async-start | bytes 5013504 | tf_op jit(solution)/shard_map/all_gather | solution.py:99
  51.9 19.0 %copy-start.4 = (bf16[96,2304]{1,0:T(8,128)(2,1)S(1)}, bf16[96,2304]{1,0:T(8,128)(2,1)}, u32[]{:S(2)}) copy-start(bf16[96,2304]{1,0:T(8,128)(2,1)} %param.11) | copy-start | bytes 1327108
  51.9 65.6 %copy-start.2 = (bf16[2,16,2304]{2,1,0:T(8,128)(2,1)S(1)}, bf16[2,16,2304]{2,1,0:T(8,128)(2,1)}, u32[]{:S(2)}) copy-start(bf16[2,16,2304]{2,1,0:T(8,128)(2,1)} %param.9) | copy-start | bytes 442372
  61.4 57.3 %copy-start.5 = (f32[2,2304]{1,0:T(2,128)S(1)}, f32[2,2304]{1,0:T(2,128)}, u32[]{:S(2)}) copy-start(f32[2,2304]{1,0:T(2,128)} %param.10) | copy-start | bytes 55300
  126.7 20.6 %copy-start.6 = (u32[32]{0:T(128)S(1)}, u32[32]{0:T(128)}, u32[]{:S(2)}) copy-start(u32[32]{0:T(128)} %constant.33) | copy-start | bytes 388
  161.5 60.3 %copy-start.3 = (bf16[2,16,2304]{2,1,0:T(8,128)(2,1)S(1)}, bf16[2,16,2304]{2,1,0:T(8,128)(2,1)}, u32[]{:S(2)}) copy-start(bf16[2,16,2304]{2,1,0:T(8,128)(2,1)} %get-tuple-element.13) | copy-start | bytes 442372
  208.4 14.5 %collective-permute-start.2 = (f32[16,2304]{1,0:T(8,128)S(1)}, f32[16,2304]{1,0:T(8,128)S(1)}, u32[]{:S(2)}, u32[]{:S(2)}) collective-permute-start(f32[16,2304]{1,0:T(8,128)S(1)} %fusion), channel_id=1, source_target_pairs={{0,6},{2,8},{4,10},{6,12},{8,14},{10,16},{12,18},{14,20},{16,22},{... | collective-permute-start | bytes 442376
  209.7 13.2 %collective-permute-start.1 = (f32[16,2304]{1,0:T(8,128)S(1)}, f32[16,2304]{1,0:T(8,128)S(1)}, u32[]{:S(2)}, u32[]{:S(2)}) collective-permute-start(f32[16,2304]{1,0:T(8,128)S(1)} %fusion), channel_id=1, source_target_pairs={{0,4},{2,6},{4,8},{6,10},{8,12},{10,14},{12,16},{14,18},{16,20},{1... | collective-permute-start | bytes 442376
  212.5 10.5 %collective-permute-start = (f32[16,2304]{1,0:T(8,128)S(1)}, f32[16,2304]{1,0:T(8,128)S(1)}, u32[]{:S(2)}, u32[]{:S(2)}) collective-permute-start(f32[16,2304]{1,0:T(8,128)S(1)} %fusion), channel_id=1, source_target_pairs={{0,2},{2,4},{4,6},{6,8},{8,10},{10,12},{12,14},{14,16},{16,18},{18... | collective-permute-start | bytes 442376
  215.4 7.5 %collective-permute-start.3 = (f32[12,2304]{1,0:T(8,128)S(1)}, f32[12,2304]{1,0:T(8,128)S(1)}, u32[]{:S(2)}, u32[]{:S(2)}) collective-permute-start(f32[12,2304]{1,0:T(8,128)S(1)} %slice.20), channel_id=1, source_target_pairs={{0,8},{2,10},{4,12},{6,14},{8,16},{10,18},{12,20},{14,22},{16,24},... | collective-permute-start | bytes 331784
Sparse Core Ops, SparseCore 0:
  51.5 66.0 all-reduce.5
  147.4 68.1 all-gather.3
